TPU v7x, 32 devices: a whole 2x2x4 slice. The times are simulated.
32 devices in a mesh: grp: 4 (over z), ctx: 2 (over y), wid: 4 (over x, core).
Axes of the slice: x: 2, y: 2, z: 4, core: 2. Of those that a mesh axis runs over, the one named last changes fastest.
Arguments:
- query: bfloat16 [256, 64, 128], P(None, 'wid'), may hold values from -64 to 64
- keys: bfloat16 [4, 512, 8, 128], P(None, ('grp', 'ctx'), 'wid'), may hold values from -64 to 64
- values: bfloat16 [4, 512, 8, 128], P(None, ('grp', 'ctx'), 'wid'), may hold values from -6 to 6
- lengths: int32 [4, 8], replicated, may hold values from 32 to 64
- query_pos: int32 [256], replicated, may hold values from 128 to 511
- resid: bfloat16 [256, 5120], P('wid', ('grp', 'ctx')), may hold values from -1.1953125 to 1.1953125
- out_weight: bfloat16 [8192, 5120], P('wid', ('grp', 'ctx')), may hold values from -0.0625 to 0.0625
- enc_weight: bfloat16 [5120, 24576], P('wid', ('grp', 'ctx')), may hold values from -0.078125 to 0.078125
- enc_bias: float32 [24576], P(('grp', 'ctx')), may hold values from -3 to 3
- dec_weight: bfloat16 [24576, 5120], P(('grp', 'ctx'), 'wid'), may hold values from -0.078125 to 0.078125
- dec_bias: float32 [5120], P('wid'), may hold values from -3 to 3
Outputs:
- layer_out: bfloat16 [256, 5120], P('wid', ('grp', 'ctx'))
- enc_grad: bfloat16 [5120, 24576], P('wid', ('grp', 'ctx'))
- enc_bias_grad: float32 [24576], P(('grp', 'ctx'))
- dec_grad: bfloat16 [24576, 5120], P(('grp', 'ctx'), 'wid')
- dec_bias_grad: float32 [5120], P('wid')
Inputs may be any that keep to these rules, and one draw needn't show every extreme that they name: `lengths`: live slots of a shard are its first ones.
All inputs are finite; a program needn't handle non-finite values.
Results may differ from a plain program's by a relative error of at most 0.024.
Values may be sent and summed in bfloat16 or wider, within the bound.
A program may use at most 128 MiB of HBM per device.

v0:
```python
import jax
import jax.numpy as jnp
from jax import lax
from jax.sharding import PartitionSpec as P

HD = 128


def body(
    query,
    keys,
    values,
    lengths,
    query_pos,
    resid,
    out_weight,
    enc_weight,
    enc_bias,
    dec_weight,
    dec_bias,
):
    seq_count, slot_count, kv_local, head_dim = keys.shape
    row_count = query.shape[0]
    heads_local = query.shape[1]
    group_size = heads_local // kv_local
    rows_each = row_count // seq_count
    shard_pos = lax.axis_index(("grp", "ctx"))
    shard_ids = jnp.arange(lengths.shape[1], dtype=jnp.int32)
    offset = jnp.sum(jnp.where(shard_ids[None, :] < shard_pos, lengths, 0), axis=1)
    live_count = jnp.sum(jnp.where(shard_ids[None, :] == shard_pos, lengths, 0), axis=1)
    slot_ids = jnp.arange(slot_count, dtype=jnp.int32)
    key_pos = offset[:, None] + slot_ids[None, :]
    live_slot = slot_ids[None, :] < live_count[:, None]
    row_position = query_pos.reshape(seq_count, rows_each)
    visible = live_slot[:, None, :] & (key_pos[:, None, :] <= row_position[:, :, None])
    visible_mask = visible[:, :, None, None, :]
    q_view = query.reshape(seq_count, rows_each, kv_local, group_size, head_dim)
    scores = jnp.einsum(
        "srkgd,sjkd->srkgj", q_view, keys, preferred_element_type=jnp.float32
    ) * HD ** (-0.5)
    local_peak = jnp.max(jnp.where(visible_mask, scores, -1e30), axis=-1)
    peak = lax.pmax(local_peak, ("grp", "ctx"))
    weights = jnp.where(visible_mask, jnp.exp(scores - peak[..., None]), 0.0)
    weight_sum = jnp.sum(weights, axis=-1)
    weights_low = weights.astype(jnp.bfloat16)
    weighted = jnp.einsum(
        "srkgj,sjkd->srkgd", weights_low, values, preferred_element_type=jnp.float32
    )
    weight_sum, weighted = (weight_sum, weighted)
    weight_sum, weighted = lax.psum((weight_sum, weighted), ("grp", "ctx"))
    attention = (weighted / weight_sum[..., None]).astype(jnp.bfloat16)
    attention = attention.reshape(row_count, heads_local * head_dim)
    projected = jnp.dot(attention, out_weight, preferred_element_type=jnp.float32)
    mixed = lax.psum_scatter(
        projected.astype(jnp.bfloat16), "wid", scatter_dimension=0, tiled=True
    ).astype(jnp.float32)
    layer_out = (mixed + resid.astype(jnp.float32)).astype(jnp.bfloat16)
    wide_rows = lax.all_gather(layer_out, ("grp", "ctx"), axis=1, tiled=True)
    block = lax.all_to_all(wide_rows, "wid", split_axis=1, concat_axis=0, tiled=True)
    enc_part = jnp.dot(block, enc_weight, preferred_element_type=jnp.float32)
    preact = lax.psum(enc_part.astype(jnp.bfloat16), "wid").astype(jnp.float32) + enc_bias
    latents = (jax.nn.softplus(4.0 * preact) * 0.25).astype(jnp.bfloat16)
    row_scale = row_count ** (-0.5)
    recon = lax.psum_scatter(
        jnp.dot(latents, dec_weight, preferred_element_type=jnp.float32),
        ("grp", "ctx"),
        scatter_dimension=0,
        tiled=True,
    )
    piece_len = recon.shape[0]
    target = lax.dynamic_slice_in_dim(block, shard_pos * piece_len, piece_len, 0).astype(
        jnp.float32
    )
    scaled_error = ((recon + dec_bias - target) * row_scale).astype(jnp.bfloat16)
    error_all = lax.all_gather(scaled_error, ("grp", "ctx"), axis=0, tiled=True)
    dec_bias_grad = jnp.sum(error_all, axis=0, dtype=jnp.float32)
    latent_part = lax.dot_general(
        error_all, dec_weight, (((1,), (1,)), ((), ())), preferred_element_type=jnp.float32
    )
    dec_grad = lax.dot_general(
        latents, error_all, (((0,), (0,)), ((), ())), preferred_element_type=jnp.float32
    )
    latent_grad = lax.psum(latent_part.astype(jnp.bfloat16), "wid").astype(jnp.float32)
    preact_grad = (latent_grad * jax.nn.sigmoid(4.0 * preact)).astype(jnp.bfloat16)
    enc_grad = lax.dot_general(
        block, preact_grad, (((0,), (0,)), ((), ())), preferred_element_type=jnp.float32
    ).astype(jnp.bfloat16)
    enc_bias_grad = jnp.sum(preact_grad, axis=0, dtype=jnp.float32)
    return (layer_out, enc_grad, enc_bias_grad, dec_grad.astype(jnp.bfloat16), dec_bias_grad)


def solution(mesh):
    placed = (
        P(None, "wid", None),
        P(None, ("grp", "ctx"), "wid", None),
        P(None, ("grp", "ctx"), "wid", None),
        P(),
        P(),
        P("wid", ("grp", "ctx")),
        P("wid", ("grp", "ctx")),
        P("wid", ("grp", "ctx")),
        P(("grp", "ctx")),
        P(("grp", "ctx"), "wid"),
        P("wid"),
    )
    return jax.shard_map(
        body,
        mesh=mesh,
        in_specs=placed,
        out_specs=(
            P("wid", ("grp", "ctx")),
            P("wid", ("grp", "ctx")),
            P(("grp", "ctx")),
            P(("grp", "ctx"), "wid"),
            P("wid"),
        ),
        check_vma=False,
    )
```

profile of v0, /device:TPU:0, one launch (start us, length us, event | category | flops | bytes accessed | tf_op | source)
XLA Modules:
  0.0 456.0 jit_solution(1669517848478432027)
XLA Ops:
  7.2 0.9 le.20
  8.1 0.8 select_reduce_fusion.1
  9.1 0.1 compare_and_fusion
  9.3 3.8 fusion.2
  13.0 39.0 %pmax.7 = f32[4,64,2,8]{1,3,2,0:T(8,128)S(1)} all-reduce(f32[4,64,2,8]{1,3,2,0:T(8,128)S(1)} %get-tuple-element.11), channel_id=1, replica_groups=mesh['grp'=4,'ctx'=2,'wid'=4] {'grp','ctx'}, use_global_device_ids=true, to_apply=%region_3.4 | all-reduce | flops 4096 | bytes 32768 | tf_op jit(solution)/shard_map/pmax | solution.py:42
  52.0 3.2 fusion.5
  55.3 2.4 copy.29
  57.7 3.0 convolution_bitcast_fusion
  60.7 34.2 %psum.29 = f32[4,64,2,8]{1,3,2,0:T(8,128)S(1)} all-reduce(f32[4,64,2,8]{1,3,2,0:T(8,128)S(1)} %get-tuple-element.9), channel_id=1, replica_groups=mesh['grp'=4,'ctx'=2,'wid'=4] {'grp','ctx'}, use_global_device_ids=true, to_apply=%region_6.7 | all-reduce | flops 4096 | bytes 32768 | tf_op jit(solution)/shard_map/psum | solution.py:50
  94.9 0.1 copy.31
  95.0 65.7 %all-reduce.4.cloned.1.call-done = f32[4,64,2,8,128]{4,3,1,2,0:T(8,128)} async-done(((f32[4,64,2,8,128]{4,3,1,2,0:T(8,128)}), f32[4,64,2,8,128]{4,3,1,2,0:T(8,128)}) %all-reduce.4.cloned.1.call-update) | async-done | bytes 2097168 | tf_op jit(solution)/shard_map/psum | solution.py:50
  160.8 1.9 divide_convert_fusion
  162.7 1.2 copy.32
  163.9 2.3 reshape.71
  166.2 2.9 convolution_convert_fusion.4
  169.2 19.8 %reduce-scatter.3.cloned.1.call-done = bf16[64,640]{1,0:T(8,128)(2,1)} async-done(((bf16[256,640]{1,0:T(8,128)(2,1)}), bf16[64,640]{1,0:T(8,128)(2,1)}) %reduce-scatter.3.cloned.1.call-update) | async-done | bytes 81936 | tf_op jit(solution)/shard_map/reduce_scatter | solution.py:54
  189.0 0.9 add_convert_fusion
  189.9 32.1 %all_gather.6 = bf16[64,5120]{1,0:T(8,128)(2,1)S(1)} all-gather(bf16[64,640]{1,0:T(8,128)(2,1)S(1)} %add_convert_fusion), channel_id=1, replica_groups=mesh['grp'=4,'ctx'=2,'wid'=4] {'grp','ctx'}, dimensions={1}, use_global_device_ids=true | all-gather | bytes 737280 | tf_op jit(solution)/shard_map/all_gather | solution.py:58
  222.1 12.6 %all_to_all.19 = bf16[64,4,1280]{2,0,1:T(8,128)(2,1)S(1)} all-to-all(bf16[64,4,1280]{2,0,1:T(8,128)(2,1)S(1)} %bitcast.41), channel_id=1, replica_groups=mesh['grp'=4,'ctx'=2,'wid'=4] {'wid'}, dimensions={1} | all-to-all | bytes 1310720 | tf_op jit(solution)/shard_map/all_to_all | solution.py:59
  234.7 6.6 %convolution_convert_fusion.3 = bf16[256,3072]{1,0:T(8,128)(2,1)} fusion(bf16[256,1280]{1,0:T(8,128)(2,1)S(1)} %bitcast.38, bf16[1280,3072]{1,0:T(8,128)(2,1)} %param.18), kind=kOutput, calls=%fused_computation.4 | convolution fusion | flops 2014052352 | bytes 10092544 | tf_op jit(solution)/shard_map/dot_general | solution.py:60
  241.4 42.7 %all-reduce.6.cloned.1.call-done = bf16[256,3072]{1,0:T(8,128)(2,1)} async-done(((bf16[256,3072]{1,0:T(8,128)(2,1)}), bf16[256,3072]{1,0:T(8,128)(2,1)}) %all-reduce.6.cloned.1.call-update) | async-done | bytes 1572880 | tf_op jit(solution)/shard_map/psum | solution.py:61
  284.1 8.8 %fusion.12 = f32[256,1280]{1,0:T(8,128)} fusion(bf16[3072,1280]{1,0:T(8,128)(2,1)} %param.20, bf16[256,3072]{1,0:T(8,128)(2,1)} %all-reduce.6.cloned.1.call-done, f32[3072]{0:T(1024)S(1)} %copy-done.5), kind=kOutput, calls=%fused_computation.35 | convolution fusion | flops 2021916672 | bytes 10760192 | tf_op jit(solution)/shard_map/dot_general | solution.py:65
  293.0 65.3 %reduce-scatter.5.cloned.1.call-done = f32[32,1280]{1,0:T(8,128)} async-done(((f32[256,1280]{1,0:T(8,128)}), f32[32,1280]{1,0:T(8,128)}) %reduce-scatter.5.cloned.1.call-update) | async-done | bytes 163856 | tf_op jit(solution)/shard_map/reduce_scatter | solution.py:64
  358.3 0.9 multiply_convert_fusion.1
  359.2 32.1 %all_gather.7 = bf16[256,1280]{1,0:T(8,128)(2,1)S(1)} all-gather(bf16[32,1280]{1,0:T(8,128)(2,1)S(1)} %multiply_convert_fusion.1), channel_id=1, replica_groups=mesh['grp'=4,'ctx'=2,'wid'=4] {'grp','ctx'}, dimensions={0}, use_global_device_ids=true | all-gather | bytes 737280 | tf_op jit(solution)/shard_map/all_gather | solution.py:75
  391.4 0.8 copy-done.1
  392.2 6.6 %convolution_convert_fusion.2 = bf16[256,3072]{1,0:T(8,128)(2,1)} fusion(bf16[256,1280]{1,0:T(8,128)(2,1)S(1)} %all_gather.7, bf16[3072,1280]{1,0:T(8,128)(2,1)} %param.20), kind=kOutput, calls=%fused_computation.3 | convolution fusion | flops 2014052352 | bytes 10092544 | tf_op jit(solution)/shard_map/dot_general | solution.py:77
  398.8 1.8 convert_reduce_fusion.1
  400.6 9.0 %convolution_convert_fusion = bf16[3072,1280]{1,0:T(8,128)(2,1)} fusion(bf16[256,1280]{1,0:T(8,128)(2,1)} %copy-done.1, bf16[256,3072]{1,0:T(8,128)(2,1)} %all-reduce.6.cloned.1.call-done, f32[3072]{0:T(1024)S(1)} %copy-done.5), kind=kOutput, calls=%fused_computation | convolution fusion | flops 2025848832 | bytes 10104832 | tf_op jit(solution)/shard_map/dot_general | solution.py:80
  409.6 30.8 %all-reduce.8.cloned.1.call-done = bf16[256,3072]{1,0:T(8,128)(2,1)} async-done(((bf16[256,3072]{1,0:T(8,128)(2,1)}), bf16[256,3072]{1,0:T(8,128)(2,1)}) %all-reduce.8.cloned.1.call-update) | async-done | bytes 1572880 | tf_op jit(solution)/shard_map/psum | solution.py:83
  440.4 3.6 convert_reduce_fusion
  444.0 5.5 %convolution_convert_fusion.1 = bf16[1280,3072]{1,0:T(8,128)(2,1)} fusion(bf16[256,1280]{1,0:T(8,128)(2,1)S(1)} %bitcast.40, bf16[256,3072]{1,0:T(8,128)(2,1)S(1)} %get-tuple-element.8), kind=kOutput, calls=%fused_computation.1 | convolution fusion | flops 2017198080 | bytes 10092544 | tf_op jit(solution)/shard_map/dot_general | solution.py:85
  (27 shorter events, 0.5 us)
Async XLA Ops:
  7.2 159.0 %copy-start = (bf16[2048,640]{1,0:T(8,128)(2,1)S(1)}, bf16[2048,640]{1,0:T(8,128)(2,1)}, u32[]{:S(2)}) copy-start(bf16[2048,640]{1,0:T(8,128)(2,1)} %param.17) | copy-start | bytes 7864324
  7.2 153.6 %all-reduce.4.cloned.1.call-start = ((), (), s32[]{:S(2)}) async-start(), calls=%async_computation.3 | async-start | bytes 4194304 | tf_op jit(solution)/shard_map/psum | solution.py:50
  13.0 44.6 %copy-start.3 = (bf16[4,64,2,128]{3,2,1,0:T(2,128)(2,1)S(1)}, bf16[4,64,2,128]{3,2,1,0:T(2,128)(2,1)}, u32[]{:S(2)}) copy-start(bf16[4,64,2,128]{3,2,1,0:T(2,128)(2,1)} %param.13) | copy-start | bytes 393220
  60.7 128.4 %reduce-scatter.3.cloned.1.call-start = ((), (), s32[]{:S(2)}) async-start(), calls=%async_computation.4 | async-start | bytes 409600 | tf_op jit(solution)/shard_map/reduce_scatter | solution.py:54
  163.9 25.1 %copy-start.4 = (bf16[64,640]{1,0:T(8,128)(2,1)S(1)}, bf16[64,640]{1,0:T(8,128)(2,1)}, u32[]{:S(2)}) copy-start(bf16[64,640]{1,0:T(8,128)(2,1)} %param.16) | copy-start | bytes 245764
  169.1 114.9 %all-reduce.6.cloned.1.call-start = ((), (), s32[]{:S(2)}) async-start(), calls=%async_computation.5 | async-start | bytes 3145728 | tf_op jit(solution)/shard_map/psum | solution.py:61
  189.9 51.4 %copy-start.2 = (bf16[64,640]{1,0:T(8,128)(2,1)}, bf16[64,640]{1,0:T(8,128)(2,1)S(1)}, u32[]{:S(2)}) copy-start(bf16[64,640]{1,0:T(8,128)(2,1)S(1)} %add_convert_fusion) | copy-start | bytes 245764
  234.7 49.3 %copy-start.5 = (f32[3072]{0:T(1024)S(1)}, f32[3072]{0:T(1024)}, u32[]{:S(2)}) copy-start(f32[3072]{0:T(1024)} %param.19) | copy-start | bytes 36868
  241.4 116.9 %copy-start.6 = (f32[1280]{0:T(1024)S(1)}, f32[1280]{0:T(1024)}, u32[]{:S(2)}) copy-start(f32[1280]{0:T(1024)} %param.21) | copy-start | bytes 15364
  241.4 116.9 %reduce-scatter.5.cloned.1.call-start = ((), (), s32[]{:S(2)}) async-start(), calls=%async_computation.6 | async-start | bytes 1474560 | tf_op jit(solution)/shard_map/reduce_scatter | solution.py:64
  293.0 147.5 %all-reduce.8.cloned.1.call-start = ((), (), s32[]{:S(2)}) async-start(), calls=%async_computation.7 | async-start | bytes 3145728 | tf_op jit(solution)/shard_map/psum | solution.py:83
  391.4 0.8 copy-start.1
Sparse Core Ops, SparseCore 0:
  60.8 99.9 all-reduce.3
  169.3 19.6 reduce-scatter.2
  241.5 42.5 all-reduce.5
  293.1 65.1 reduce-scatter.4
  398.9 41.4 all-reduce.7
where the time goes:
time: 457 us; the launch traced here: 456 us
  waiting for transfers between devices  224 us (49%)
  blocking collectives  150 us (33%)
  matrix products  46.2 us (10%)
  between operations  13.9 us (3%)
  other arithmetic  13.5 us (3%)
  local copies, waits for them, and re-layouts  7.82 us (2%)
    psum x1, waiting for transfers between devices, body(): weight_sum, weighted = lax.psum((weight_sum, weighted), ('grp', 'ctx'))  65.7 us
    reduce_scatter x1, waiting for transfers between devices, body(): lax.psum_scatter(jnp.dot(latents, dec_weight, preferred_element_type=jnp....  65.3 us
    psum x1, waiting for transfers between devices, body(): lax.psum(enc_part.astype(jnp.bfloat16), 'wid').astype(jnp.float32)  42.7 us
    pmax x1, blocking collectives, body(): peak = lax.pmax(local_peak, ('grp', 'ctx'))  39 us
    psum x1, blocking collectives, body(): weight_sum, weighted = lax.psum((weight_sum, weighted), ('grp', 'ctx'))  34.2 us
    all_gather x1, blocking collectives, body(): wide_rows = lax.all_gather(layer_out, ('grp', 'ctx'), axis=1, tiled=True)  32.1 us
    all_gather x1, blocking collectives, body(): error_all = lax.all_gather(scaled_error, ('grp', 'ctx'), axis=0, tiled=True)  32.1 us
    psum x1, waiting for transfers between devices, body(): lax.psum(latent_part.astype(jnp.bfloat16), 'wid').astype(jnp.float32)  30.8 us
  transfers between devices with their start and end apart: 5, of which 5 were waited for; matrix products, arithmetic and copies ran while one was open for 2% of the time, Pallas kernels for 0%

commit v1 on v0

--- a/solution.py
+++ b/solution.py
@@ -55,7 +55,8 @@
         projected.astype(jnp.bfloat16), "wid", scatter_dimension=0, tiled=True
     ).astype(jnp.float32)
     layer_out = (mixed + resid.astype(jnp.float32)).astype(jnp.bfloat16)
-    wide_rows = lax.all_gather(layer_out, ("grp", "ctx"), axis=1, tiled=True)
+    shards = lax.all_gather(layer_out, ("grp", "ctx"), axis=0, tiled=False)
+    wide_rows = jnp.concatenate(shards, axis=1)
     block = lax.all_to_all(wide_rows, "wid", split_axis=1, concat_axis=0, tiled=True)
     enc_part = jnp.dot(block, enc_weight, preferred_element_type=jnp.float32)
     preact = lax.psum(enc_part.astype(jnp.bfloat16), "wid").astype(jnp.float32) + enc_bias

time: 457 us -> 460 us (level)
  no operation moved by 1% of the time
where the time goes in v1:
time: 460 us; the launch traced here: 459 us
  waiting for transfers between devices  225 us (49%)
  blocking collectives  150 us (33%)
  matrix products  46.2 us (10%)
  between operations  13.9 us (3%)
  other arithmetic  13.5 us (3%)
  local copies, waits for them, and re-layouts  10.6 us (2%)
    psum x1, waiting for transfers between devices, body(): weight_sum, weighted = lax.psum((weight_sum, weighted), ('grp', 'ctx'))  65.7 us
    reduce_scatter x1, waiting for transfers between devices, body(): lax.psum_scatter(jnp.dot(latents, dec_weight, preferred_element_type=jnp....  65.3 us
    psum x1, waiting for transfers between devices, body(): lax.psum(enc_part.astype(jnp.bfloat16), 'wid').astype(jnp.float32)  43.1 us
    pmax x1, blocking collectives, body(): peak = lax.pmax(local_peak, ('grp', 'ctx'))  39 us
    psum x1, blocking collectives, body(): weight_sum, weighted = lax.psum((weight_sum, weighted), ('grp', 'ctx'))  34.2 us
    all_gather x1, blocking collectives, body(): error_all = lax.all_gather(scaled_error, ('grp', 'ctx'), axis=0, tiled=True)  32.2 us
    all_gather x1, blocking collectives, body(): shards = lax.all_gather(layer_out, ('grp', 'ctx'), axis=0, tiled=False)  31.8 us
    psum x1, waiting for transfers between devices, body(): lax.psum(latent_part.astype(jnp.bfloat16), 'wid').astype(jnp.float32)  30.7 us
  transfers between devices with their start and end apart: 5, of which 5 were waited for; matrix products, arithmetic and copies ran while one was open for 2% of the time, Pallas kernels for 0%

profile of v1, /device:TPU:0, one launch (start us, length us, event | category | flops | bytes accessed | tf_op | source)
XLA Modules:
  0.0 458.8 jit_solution(13159831020779658017)
XLA Ops:
  7.2 0.9 le.20
  8.1 0.8 select_reduce_fusion.1
  9.3 3.8 fusion.2
  13.0 39.0 %pmax.7 = f32[4,64,2,8]{1,3,2,0:T(8,128)S(1)} all-reduce(f32[4,64,2,8]{1,3,2,0:T(8,128)S(1)} %get-tuple-element.11), channel_id=1, replica_groups=mesh['grp'=4,'ctx'=2,'wid'=4] {'grp','ctx'}, use_global_device_ids=true, to_apply=%region_3.4 | all-reduce | flops 4096 | bytes 32768 | tf_op jit(solution)/shard_map/pmax | solution.py:42
  52.0 3.2 fusion.5
  55.3 2.4 copy.29
  57.7 3.0 convolution_bitcast_fusion
  60.7 34.2 %psum.29 = f32[4,64,2,8]{1,3,2,0:T(8,128)S(1)} all-reduce(f32[4,64,2,8]{1,3,2,0:T(8,128)S(1)} %get-tuple-element.9), channel_id=1, replica_groups=mesh['grp'=4,'ctx'=2,'wid'=4] {'grp','ctx'}, use_global_device_ids=true, to_apply=%region_6.7 | all-reduce | flops 4096 | bytes 32768 | tf_op jit(solution)/shard_map/psum | solution.py:50
  95.0 65.7 %all-reduce.4.cloned.1.call-done = f32[4,64,2,8,128]{4,3,1,2,0:T(8,128)} async-done(((f32[4,64,2,8,128]{4,3,1,2,0:T(8,128)}), f32[4,64,2,8,128]{4,3,1,2,0:T(8,128)}) %all-reduce.4.cloned.1.call-update) | async-done | bytes 2097168 | tf_op jit(solution)/shard_map/psum | solution.py:50
  160.8 1.9 divide_convert_fusion
  162.7 1.2 copy.32
  163.9 2.3 reshape.76
  166.2 2.9 convolution_convert_fusion.4
  169.2 19.8 %reduce-scatter.3.cloned.1.call-done = bf16[64,640]{1,0:T(8,128)(2,1)} async-done(((bf16[256,640]{1,0:T(8,128)(2,1)}), bf16[64,640]{1,0:T(8,128)(2,1)}) %reduce-scatter.3.cloned.1.call-update) | async-done | bytes 81936 | tf_op jit(solution)/shard_map/reduce_scatter | solution.py:54
  189.0 0.9 add_convert_fusion
  189.9 31.8 %all-gather = bf16[512,640]{1,0:T(8,128)(2,1)S(1)} all-gather(bf16[64,640]{1,0:T(8,128)(2,1)S(1)} %add_convert_fusion), channel_id=2, replica_groups=mesh['grp'=4,'ctx'=2,'wid'=4] {'grp','ctx'}, dimensions={0}, use_global_device_ids=true | all-gather | bytes 737280 | tf_op jit(solution)/shard_map/all_gather | solution.py:58
  222.1 1.3 all_to_all.14
  223.3 1.2 copy.34
  224.5 12.6 %all_to_all.19 = bf16[64,4,1280]{2,0,1:T(8,128)(2,1)S(1)} all-to-all(bf16[64,4,1280]{2,0,1:T(8,128)(2,1)S(1)} %copy.34), channel_id=1, replica_groups=mesh['grp'=4,'ctx'=2,'wid'=4] {'wid'}, dimensions={1} | all-to-all | bytes 1310720 | tf_op jit(solution)/shard_map/all_to_all | solution.py:60
  237.1 6.6 %convolution_convert_fusion.3 = bf16[256,3072]{1,0:T(8,128)(2,1)} fusion(bf16[256,1280]{1,0:T(8,128)(2,1)S(1)} %bitcast.38, bf16[1280,3072]{1,0:T(8,128)(2,1)} %param.18), kind=kOutput, calls=%fused_computation.4 | convolution fusion | flops 2014052352 | bytes 10092544 | tf_op jit(solution)/shard_map/dot_general | solution.py:61
  243.8 43.1 %all-reduce.6.cloned.1.call-done = bf16[256,3072]{1,0:T(8,128)(2,1)} async-done(((bf16[256,3072]{1,0:T(8,128)(2,1)}), bf16[256,3072]{1,0:T(8,128)(2,1)}) %all-reduce.6.cloned.1.call-update) | async-done | bytes 1572880 | tf_op jit(solution)/shard_map/psum | solution.py:62
  286.9 8.8 %fusion.12 = f32[256,1280]{1,0:T(8,128)} fusion(bf16[3072,1280]{1,0:T(8,128)(2,1)} %param.20, bf16[256,3072]{1,0:T(8,128)(2,1)} %all-reduce.6.cloned.1.call-done, f32[3072]{0:T(1024)S(1)} %copy-done.5), kind=kOutput, calls=%fused_computation.35 | convolution fusion | flops 2021916672 | bytes 10760192 | tf_op jit(solution)/shard_map/dot_general | solution.py:66
  295.8 65.3 %reduce-scatter.5.cloned.1.call-done = f32[32,1280]{1,0:T(8,128)} async-done(((f32[256,1280]{1,0:T(8,128)}), f32[32,1280]{1,0:T(8,128)}) %reduce-scatter.5.cloned.1.call-update) | async-done | bytes 163856 | tf_op jit(solution)/shard_map/reduce_scatter | solution.py:65
  361.1 0.9 multiply_convert_fusion.1
  362.0 32.2 %all_gather.11 = bf16[256,1280]{1,0:T(8,128)(2,1)S(1)} all-gather(bf16[32,1280]{1,0:T(8,128)(2,1)S(1)} %multiply_convert_fusion.1), channel_id=1, replica_groups=mesh['grp'=4,'ctx'=2,'wid'=4] {'grp','ctx'}, dimensions={0}, use_global_device_ids=true | all-gather | bytes 737280 | tf_op jit(solution)/shard_map/all_gather | solution.py:76
  394.2 0.8 copy-done.1
  395.0 6.6 %convolution_convert_fusion.2 = bf16[256,3072]{1,0:T(8,128)(2,1)} fusion(bf16[256,1280]{1,0:T(8,128)(2,1)S(1)} %all_gather.11, bf16[3072,1280]{1,0:T(8,128)(2,1)} %param.20), kind=kOutput, calls=%fused_computation.3 | convolution fusion | flops 2014052352 | bytes 10092544 | tf_op jit(solution)/shard_map/dot_general | solution.py:78
  401.7 1.8 convert_reduce_fusion.1
  403.4 9.0 %convolution_convert_fusion = bf16[3072,1280]{1,0:T(8,128)(2,1)} fusion(bf16[256,1280]{1,0:T(8,128)(2,1)} %copy-done.1, bf16[256,3072]{1,0:T(8,128)(2,1)} %all-reduce.6.cloned.1.call-done, f32[3072]{0:T(1024)S(1)} %copy-done.5), kind=kOutput, calls=%fused_computation | convolution fusion | flops 2025848832 | bytes 10104832 | tf_op jit(solution)/shard_map/dot_general | solution.py:81
  412.5 30.7 %all-reduce.8.cloned.1.call-done = bf16[256,3072]{1,0:T(8,128)(2,1)} async-done(((bf16[256,3072]{1,0:T(8,128)(2,1)}), bf16[256,3072]{1,0:T(8,128)(2,1)}) %all-reduce.8.cloned.1.call-update) | async-done | bytes 1572880 | tf_op jit(solution)/shard_map/psum | solution.py:84
  443.2 3.6 convert_reduce_fusion
  446.8 5.5 %convolution_convert_fusion.1 = bf16[1280,3072]{1,0:T(8,128)(2,1)} fusion(bf16[256,1280]{1,0:T(8,128)(2,1)S(1)} %bitcast.40, bf16[256,3072]{1,0:T(8,128)(2,1)S(1)} %get-tuple-element.8), kind=kOutput, calls=%fused_computation.1 | convolution fusion | flops 2017198080 | bytes 10092544 | tf_op jit(solution)/shard_map/dot_general | solution.py:86
  (29 shorter events, 1.1 us)
Async XLA Ops:
  7.2 159.0 %copy-start = (bf16[2048,640]{1,0:T(8,128)(2,1)S(1)}, bf16[2048,640]{1,0:T(8,128)(2,1)}, u32[]{:S(2)}) copy-start(bf16[2048,640]{1,0:T(8,128)(2,1)} %param.17) | copy-start | bytes 7864324
  7.2 153.6 %all-reduce.4.cloned.1.call-start = ((), (), s32[]{:S(2)}) async-start(), calls=%async_computation.3 | async-start | bytes 4194304 | tf_op jit(solution)/shard_map/psum | solution.py:50
  13.0 44.6 %copy-start.3 = (bf16[4,64,2,128]{3,2,1,0:T(2,128)(2,1)S(1)}, bf16[4,64,2,128]{3,2,1,0:T(2,128)(2,1)}, u32[]{:S(2)}) copy-start(bf16[4,64,2,128]{3,2,1,0:T(2,128)(2,1)} %param.13) | copy-start | bytes 393220
  60.7 128.4 %reduce-scatter.3.cloned.1.call-start = ((), (), s32[]{:S(2)}) async-start(), calls=%async_computation.4 | async-start | bytes 409600 | tf_op jit(solution)/shard_map/reduce_scatter | solution.py:54
  163.9 25.1 %copy-start.4 = (bf16[64,640]{1,0:T(8,128)(2,1)S(1)}, bf16[64,640]{1,0:T(8,128)(2,1)}, u32[]{:S(2)}) copy-start(bf16[64,640]{1,0:T(8,128)(2,1)} %param.16) | copy-start | bytes 245764
  169.1 117.7 %all-reduce.6.cloned.1.call-start = ((), (), s32[]{:S(2)}) async-start(), calls=%async_computation.5 | async-start | bytes 3145728 | tf_op jit(solution)/shard_map/psum | solution.py:62
  189.9 53.8 %copy-start.2 = (bf16[64,640]{1,0:T(8,128)(2,1)}, bf16[64,640]{1,0:T(8,128)(2,1)S(1)}, u32[]{:S(2)}) copy-start(bf16[64,640]{1,0:T(8,128)(2,1)S(1)} %add_convert_fusion) | copy-start | bytes 245764
  237.1 49.7 %copy-start.5 = (f32[3072]{0:T(1024)S(1)}, f32[3072]{0:T(1024)}, u32[]{:S(2)}) copy-start(f32[3072]{0:T(1024)} %param.19) | copy-start | bytes 36868
  243.7 117.3 %copy-start.6 = (f32[1280]{0:T(1024)S(1)}, f32[1280]{0:T(1024)}, u32[]{:S(2)}) copy-start(f32[1280]{0:T(1024)} %param.21) | copy-start | bytes 15364
  243.7 117.3 %reduce-scatter.5.cloned.1.call-start = ((), (), s32[]{:S(2)}) async-start(), calls=%async_computation.6 | async-start | bytes 1474560 | tf_op jit(solution)/shard_map/reduce_scatter | solution.py:65
  295.7 147.5 %all-reduce.8.cloned.1.call-start = ((), (), s32[]{:S(2)}) async-start(), calls=%async_computation.7 | async-start | bytes 3145728 | tf_op jit(solution)/shard_map/psum | solution.py:84
  394.2 0.8 copy-start.1
Sparse Core Ops, SparseCore 0:
  60.8 99.9 all-reduce.3
  169.3 19.6 reduce-scatter.2
  243.8 42.9 all-reduce.5
  295.8 65.1 reduce-scatter.4
  401.8 41.3 all-reduce.7
